TPU v7x, 32 devices: a whole 2x2x4 slice. The times are simulated.
32 devices in a mesh: light: 4 (over y, x), screen: 8 (over z, core).
Axes of the slice: x: 2, y: 2, z: 4, core: 2. Of those that a mesh axis runs over, the one named last changes fastest.
Arguments:
- density: float32 [128, 256, 512], P('screen', None, 'light'), may hold values from 0 to 1.09375, as said below
- albedo: float32 [128, 256, 512], P('screen', None, 'light'), may hold values from 0.2 to 1
- light_in: float32 [128, 256], replicated, may hold values from 0.5 to 1.5
- occupancy: int32 [8, 16, 32], P('screen', None, 'light'), may hold values 0 or 1
- phase: int32 [256, 512], replicated, may hold values from 0 to 15
- fractions: float32 [3, 16], replicated, may hold values from 0 to 1
Outputs:
- image: float32 [256, 512], P('screen', 'light')
- transmittance: float32 [256, 512], P('screen', 'light')
- lit_bricks: float32 [128, 256, 512], P('light', 'screen')
Inputs may be any that keep to these rules, and one draw needn't show every extreme that they name: `density`: nonnegative extinction of each cell. `occupancy`: 1 where the brick of 16 cells on a side is occupied.
All inputs are finite; a program needn't handle non-finite values. No bound on the sum of `occupancy` on one device may be relied on, other than what follows from the above.
Results may differ from a plain program's by a relative error of at most 0.0003.
Values sent between devices are 32-bit elements; how exact they have to be, the bound alone decides.
No kernel may reach another device: no remote copies, remote signals or barrier semaphores. Data moves between devices by JAX's collectives and lax.ppermute only.
A program may use at most 192 MiB of HBM per device.

v0:
```python
import jax
import jax.numpy as jnp
from jax import lax
from jax.sharding import PartitionSpec as P

BRICK = 16


def passed_along(value, axis, by):
    peers = lax.axis_size(axis)
    pairs = [(i, i + by) for i in range(peers) if 0 <= i + by < peers]
    return lax.ppermute(value, axis, pairs)


def carried_in(part, axis, combine, identity):
    place = lax.axis_index(axis)
    gathered = lax.all_gather(part, axis)
    state = jnp.zeros_like(part) + jnp.asarray(identity, part.dtype)

    def one(step, state):
        return combine(state, lax.dynamic_index_in_dim(gathered, step, 0, False))

    return lax.fori_loop(0, place, one, state)


def prefix_last(values):
    length = values.shape[-1]
    block = 128
    count = length // block
    shaped = values.reshape(values.shape[:-1] + (count, block))
    rowsidx = lax.broadcasted_iota(jnp.int32, (block, block), 0)
    colsidx = lax.broadcasted_iota(jnp.int32, (block, block), 1)
    upper = (rowsidx < colsidx).astype(jnp.float32)
    within = jnp.matmul(shaped, upper, precision=lax.Precision.HIGHEST)
    totals = jnp.sum(shaped, axis=-1)
    carried = jnp.cumsum(totals, axis=-1) - totals
    return (within + carried[..., None]).reshape(values.shape)


def prefix_first(values):
    length = values.shape[0]
    count = length // length
    shaped = values.reshape(count, length, -1)
    rowsidx = lax.broadcasted_iota(jnp.int32, (length, length), 0)
    colsidx = lax.broadcasted_iota(jnp.int32, (length, length), 1)
    lower = (colsidx < rowsidx).astype(jnp.float32)
    within = jnp.einsum("ij,bjr->bir", lower, shaped, precision=lax.Precision.HIGHEST)
    totals = jnp.sum(shaped, axis=1)
    carried = jnp.cumsum(totals, axis=0) - totals
    return (within + carried[:, None]).reshape(values.shape)


def corner_fractions(rays, fractions):
    levels = lax.broadcasted_iota(jnp.int32, (fractions.shape[1], 1, 1), 0)
    onehot = (rays[None] == levels).astype(jnp.float32)
    return jnp.einsum("kp,prc->krc", fractions, onehot, precision=lax.Precision.HIGHEST)


def resample(field, tail, weights, deep, cols):
    first = field[:, 0:cols]
    second = field[:, 1 : cols + 1]
    edge_first = tail[:, 0:cols]
    edge_second = tail[:, 1 : cols + 1]
    first_next = jnp.concatenate([first[:, :, 1:], edge_first], axis=2)
    second_next = jnp.concatenate([second[:, :, 1:], edge_second], axis=2)
    depth_w = weights[0]
    column_w = weights[1]
    light_w = weights[2]
    near = first + column_w * (second - first)
    further = first_next + column_w * (second_next - first_next)
    mixed = near + light_w * (further - near)
    lower = mixed[0:deep]
    higher = mixed[1 : deep + 1]
    return lower + depth_w * (higher - lower)


def composite(extinct, shaded):
    screened = prefix_first(extinct)
    part = jnp.sum(jnp.exp(-screened) * (1.0 - jnp.exp(-extinct)) * shaded, axis=0)
    return (part, jnp.sum(extinct, axis=0))


def finish(parts, totals):
    before = jnp.cumsum(totals, axis=0) - totals
    picture = jnp.sum(jnp.exp(-before) * parts, axis=0)
    return (picture, jnp.exp(-jnp.sum(totals, axis=0)))


def march_slabs(masked, lit, phase, fractions):
    slab_b, width_a, slab_l = masked.shape
    light_idx = lax.axis_index("light")
    rims = passed_along((masked[:2], lit[:2]), "screen", -1)
    dens_ext = jnp.pad(jnp.concatenate([masked, rims[0]], axis=0), ((0, 0), (0, 2), (0, 0)))
    lit_ext = jnp.pad(jnp.concatenate([lit, rims[1]], axis=0), ((0, 0), (0, 2), (0, 0)))
    tails = passed_along((dens_ext[:, :, :1], lit_ext[:, :, :1]), "light", -1)
    rays = lax.dynamic_slice_in_dim(phase, light_idx * slab_l, slab_l, 1)
    weights = corner_fractions(rays, fractions)
    extinct = resample(dens_ext, tails[0], weights, slab_b, width_a)
    shaded = resample(lit_ext, tails[1], weights, slab_b, width_a)
    part, total = composite(extinct, shaded)
    parts, totals = (
        lax.all_to_all(part[None], "screen", split_axis=1, concat_axis=0, tiled=True),
        lax.all_to_all(total[None], "screen", split_axis=1, concat_axis=0, tiled=True),
    )
    return finish(parts, totals)


def local(density, albedo, light_in, occupancy, phase, fractions):
    slab_b, width_a, slab_l = density.shape
    bricks_b, bricks_a, bricks_l = occupancy.shape
    masked = (
        density.reshape(bricks_b, BRICK, bricks_a, BRICK, bricks_l, BRICK)
        * occupancy.astype(jnp.float32)[:, None, :, None, :, None]
    ).reshape(density.shape)
    screen_idx = lax.axis_index("screen")
    local_depth = prefix_last(masked)
    totals = jnp.sum(masked, axis=2)
    before = carried_in(totals, "light", jnp.add, jnp.zeros_like(totals))
    incoming = lax.dynamic_slice_in_dim(light_in, screen_idx * slab_b, slab_b, 0)
    lit = albedo * incoming[:, :, None] * jnp.exp(-(local_depth + before[:, :, None]))
    lit_cam = lax.all_to_all(lit, "screen", split_axis=1, concat_axis=0, tiled=True)
    lit_cam = lax.all_to_all(lit_cam, "light", split_axis=0, concat_axis=2, tiled=True)
    picture, passing = march_slabs(masked, lit, phase, fractions)
    return (picture, passing, lit_cam)


def solution(mesh):
    return jax.shard_map(
        local,
        mesh=mesh,
        in_specs=(
            P("screen", None, "light"),
            P("screen", None, "light"),
            P(),
            P("screen", None, "light"),
            P(),
            P(),
        ),
        out_specs=(P("screen", "light"), P("screen", "light"), P("light", "screen", None)),
        check_vma=False,
    )
```

profile of v0, /device:TPU:0, one launch (start us, length us, event | category | flops | bytes accessed | tf_op | source)
XLA Modules:
  0.0 195.5 jit_solution(17380704200879934052)
XLA Ops:
  0.7 0.7 convert_bitcast_fusion
  1.9 2.2 %fusion.35 = (f32[16,256]{1,0:T(8,128)S(1)}, f32[16,256,128]{2,1,0:T(8,128)S(1)}) fusion(f32[16,256,128]{2,1,0:T(8,128)} %param.8, f32[256,128]{1,0:T(8,128)S(1)} %mul.121), kind=kLoop, calls=%fused_computation.62 | loop fusion | flops 1044480 | bytes 4341760 | tf_op jit(solution)/shard_map/reduce_sum | solution.py:35
  4.2 9.7 %all-gather = f32[64,256]{1,0:T(8,128)S(1)} all-gather(f32[16,256]{1,0:T(8,128)S(1)} %get-tuple-element.35), channel_id=2, replica_groups=mesh['light'=4,'screen'=8] {'light'}, dimensions={0}, use_global_device_ids=true | all-gather | bytes 81920 | tf_op jit(solution)/shard_map/all_gather | solution.py:17
  13.9 0.7 constant_dynamic-slice_fusion
  14.6 3.8 %exponential_multiply_fusion = f32[16,256,128]{2,1,0:T(8,128)S(1)} fusion(f32[16,256,128]{2,1,0:T(8,128)} %param.9, f32[16,256,128]{2,1,0:T(8,128)S(1)} %get-tuple-element.36, f32[16,256]{1,0:T(8,128)S(1)} %get-tuple-element.26, f32[16,256]{1,0:T(8,128)S(1)} %sub.66, f32[16,256]{1,0:T(8,128)S(1)} %constant_dynamic-slice_fusion), kind=kOutput, calls=%fused_computation.42 | convolution fusion | flops 807944192 | bytes 6340608 | tf_op jit(solution)/shard_map/dot_general | solution.py:34
  18.5 1.3 copy-done.3
  19.8 1.3 collective-permute-start.2
  21.1 10.6 %reshape.82 = f32[1,16,16,16,8,16]{5,4,3,2,1,0:T(8,128)} reshape(f32[16,256,128]{2,1,0:T(8,128)} %param.8) | data formatting | bytes 4194304 | tf_op jit(solution)/shard_map/reshape | solution.py:112
  31.7 1.9 slice_multiply_fusion
  33.6 1.3 slice.74
  34.8 1.3 collective-permute-start
  36.2 0.7 fusion.27
  36.9 1.0 fusion.38
  37.9 1.7 pad_maximum_fusion.1
  39.6 2.1 %pad_slice_fusion.2 = f32[18,256,127]{2,1,0:T(8,128)} fusion(f32[18,256,128]{2,1,0:T(8,128)S(1)} %pad_maximum_fusion.1), kind=kLoop, calls=%fused_computation.25 | loop fusion | bytes 4700160 | tf_op jit(solution)/shard_map/slice | solution.py:65
  41.7 1.6 pad_slice_fusion.3
  43.4 0.9 copy-done.6
  44.4 2.2 %pad_slice_fusion.4 = f32[18,256,127]{2,1,0:T(8,128)} fusion(f32[18,256,128]{2,1,0:T(8,128)S(1)} %pad_maximum_fusion), kind=kLoop, calls=%fused_computation.27 | loop fusion | bytes 4700160 | tf_op jit(solution)/shard_map/slice | solution.py:65
  46.6 1.6 pad_slice_fusion.5
  48.2 2.7 %copy.33 = f32[18,258,1]{1,2,0:T(1,128)S(1)} copy(f32[18,258,1]{2,1,0:T(8,128)} %pad_slice_fusion.3) | data formatting | bytes 37152 | tf_op jit(solution)/shard_map/slice | solution.py:95
  50.9 1.3 collective-permute-start.3
  52.2 2.7 %copy.30 = f32[18,258,1]{1,2,0:T(1,128)S(1)} copy(f32[18,258,1]{2,1,0:T(8,128)} %pad_slice_fusion.5) | data formatting | bytes 37152 | tf_op jit(solution)/shard_map/slice | solution.py:95
  54.9 1.6 collective-permute-start.1
  56.5 3.7 %fusion.3 = f32[18,256,127]{2,1,0:T(8,128)} fusion(f32[2,256,128]{2,1,0:T(8,128)S(1)} %collective-permute-done.2, f32[16,256,128]{2,1,0:T(8,128)} %copy-done.3), kind=kLoop, calls=%fused_computation.9 | loop fusion | flops 585216 | bytes 4700160 | tf_op jit(solution)/shard_map/concatenate | solution.py:94
  60.2 2.1 %fusion.4 = f32[18,256,127]{2,1,0:T(8,128)} fusion(f32[2,256,128]{2,1,0:T(8,128)S(1)} %collective-permute-done, f32[16,256,128]{2,1,0:T(8,128)S(1)} %copy-done.7), kind=kLoop, calls=%fused_computation.10 | loop fusion | flops 585216 | bytes 4700160 | tf_op jit(solution)/shard_map/concatenate | solution.py:93
  62.4 2.1 %copy.35 = f32[18,256,1]{2,1,0:T(8,128)} copy(f32[18,256,1]{1,2,0:T(1,128)S(1)} %get-tuple-element.44) | data formatting | bytes 36864 | tf_op jit(solution)/shard_map/slice | solution.py:63
  64.6 2.2 %copy.34 = f32[18,256,1]{2,1,0:T(8,128)} copy(f32[18,256,1]{1,2,0:T(1,128)S(1)} %get-tuple-element.45) | data formatting | bytes 36864 | tf_op jit(solution)/shard_map/slice | solution.py:62
  66.8 2.1 %copy.32 = f32[18,256,1]{2,1,0:T(8,128)} copy(f32[18,256,1]{1,2,0:T(1,128)S(1)} %get-tuple-element.46) | data formatting | bytes 36864 | tf_op jit(solution)/shard_map/slice | solution.py:63
  69.0 2.1 %copy.31 = f32[18,256,1]{2,1,0:T(8,128)} copy(f32[18,256,1]{1,2,0:T(1,128)S(1)} %get-tuple-element.47) | data formatting | bytes 36864 | tf_op jit(solution)/shard_map/slice | solution.py:62
  71.1 12.0 %fusion.14 = (f32[18,256,128]{2,1,0:T(8,128)}, f32[18,256,128]{2,1,0:T(8,128)S(1)}) fusion(f32[18,256,1]{2,1,0:T(8,128)} %copy.34, f32[18,256,127]{2,1,0:T(8,128)} %fusion.3, f32[18,256,1]{2,1,0:T(8,128)} %copy.35, f32[18,256,127]{2,1,0:T(8,128)} %pad_slice_fusion.2, f32[18,256,128]{2,1,0:T(8,128)S(1)} %pad_maximum_fusion.1, f32[256,128]{1,0:T(8,128)S(1)} %bitcast.74, ...), kind=kLoop, calls=%fused_computation.24 | loop fusion | flops 12976128 | bytes 19136512 | tf_op jit(solution)/shard_map/add | solution.py:71
  83.2 2.3 %fusion.36 = (f32[256,128]{1,0:T(8,128)}, f32[16,256,128]{2,1,0:T(8,128)}) fusion(f32[18,256,128]{2,1,0:T(8,128)S(1)} %get-tuple-element.43, f32[256,128]{1,0:T(8,128)S(1)} %bitcast.72), kind=kLoop, calls=%fused_computation.63 | loop fusion | flops 2064384 | bytes 6553600 | tf_op jit(solution)/shard_map/reduce_sum | solution.py:80
  85.5 6.7 %all-to-all-start = ((f32[1,256,128]{2,0,1:T(1,128)}), f32[1,256,128]{2,0,1:T(1,128)S(1)}, u32[]{:S(2)}, u32[]{:S(2)}) async-start(f32[1,256,128]{2,0,1:T(1,128)} %bitcast.7), calls=%async_computation | async-start | bytes 262144 | tf_op jit(solution)/shard_map/all_to_all | solution.py:103
  92.2 2.5 %copy.36 = f32[16,256,128]{2,0,1:T(8,128)} copy(f32[16,256,128]{2,1,0:T(8,128)S(1)} %copy-done.4) | data formatting | bytes 4194304 | tf_op jit(solution)/shard_map/mul | solution.py:120
  94.7 4.2 %all-to-all-done = f32[1,256,128]{2,0,1:T(1,128)S(1)} async-done(((f32[1,256,128]{2,0,1:T(1,128)}), f32[1,256,128]{2,0,1:T(1,128)S(1)}, u32[]{:S(2)}, u32[]{:S(2)}) %all-to-all-start) | async-done | bytes 131104 | tf_op jit(solution)/shard_map/all_to_all | solution.py:103
  98.9 4.4 %all-to-all-start.2 = ((f32[16,256,128]{2,0,1:T(8,128)}), f32[16,256,128]{2,0,1:T(8,128)}, u32[]{:S(2)}, u32[]{:S(2)}) async-start(f32[16,256,128]{2,0,1:T(8,128)} %copy.36), calls=%async_computation.2 | async-start | bytes 4194304 | tf_op jit(solution)/shard_map/all_to_all | solution.py:121
  103.3 0.9 subtract_bitcast_fusion
  104.2 2.5 %fusion.24 = f32[2,8,256,128]{3,1,2,0:T(8,128)S(1)} fusion(f32[2,8,256,128]{3,2,1,0:T(8,128)S(1)} %bitcast.67, f32[32768]{0:T(1024)S(1)} %subtract_bitcast_fusion), kind=kOutput, calls=%fused_computation.45 | convolution fusion | flops 101712128 | bytes 4325376 | tf_op jit(solution)/shard_map/ij,bjr->bir/dot_general | solution.py:47
  107.1 1.2 copy-done.9
  108.4 1.3 fusion.16
  109.7 42.7 %all-to-all-done.2 = f32[16,256,128]{2,0,1:T(8,128)} async-done(((f32[16,256,128]{2,0,1:T(8,128)}), f32[16,256,128]{2,0,1:T(8,128)}, u32[]{:S(2)}, u32[]{:S(2)}) %all-to-all-start.2) | async-done | bytes 2097184 | tf_op jit(solution)/shard_map/all_to_all | solution.py:121
  152.3 3.4 %all-to-all-start.1 = ((f32[1,256,128]{2,0,1:T(1,128)}), f32[1,256,128]{2,0,1:T(1,128)S(1)}, u32[]{:S(2)}, u32[]{:S(2)}) async-start(f32[1,256,128]{2,0,1:T(1,128)} %bitcast.14), calls=%async_computation.1 | async-start | bytes 262144 | tf_op jit(solution)/shard_map/all_to_all | solution.py:102
  155.7 3.5 %copy.38 = f32[8,16,32,128]{3,2,1,0:T(8,128)} copy(f32[8,16,32,128]{3,1,2,0:T(8,128)} %bitcast.18) | data formatting | bytes 4194304 | tf_op jit(solution)/shard_map/all_to_all | solution.py:121
  159.3 3.1 %all-to-all-done.1 = f32[1,256,128]{2,0,1:T(1,128)S(1)} async-done(((f32[1,256,128]{2,0,1:T(1,128)}), f32[1,256,128]{2,0,1:T(1,128)S(1)}, u32[]{:S(2)}, u32[]{:S(2)}) %all-to-all-start.1) | async-done | bytes 131104 | tf_op jit(solution)/shard_map/all_to_all | solution.py:102
  162.4 6.9 %all-to-all-start.3 = ((f32[128,32,128]{2,1,0:T(8,128)}), f32[128,32,128]{2,1,0:T(8,128)S(1)}, u32[]{:S(2)}, u32[]{:S(2)}) async-start(f32[128,32,128]{2,1,0:T(8,128)} %bitcast.19), calls=%async_computation.3 | async-start | bytes 4194304 | tf_op jit(solution)/shard_map/all_to_all | solution.py:122
  169.4 0.6 negate_exponential_fusion
  170.0 0.6 fusion.41
  170.6 23.3 %all-to-all-done.3 = f32[128,32,128]{2,1,0:T(8,128)S(1)} async-done(((f32[128,32,128]{2,1,0:T(8,128)}), f32[128,32,128]{2,1,0:T(8,128)S(1)}, u32[]{:S(2)}, u32[]{:S(2)}) %all-to-all-start.3) | async-done | bytes 2097184 | tf_op jit(solution)/shard_map/all_to_all | solution.py:122
  193.9 1.6 copy.51
  (40 shorter events, 1.5 us)
Async XLA Ops:
  0.6 35.5 %copy-start = (s32[256,512]{1,0:T(8,128)S(1)}, s32[256,512]{1,0:T(8,128)}, u32[]{:S(2)}) copy-start(s32[256,512]{1,0:T(8,128)} %param.12) | copy-start | bytes 1572868
  4.1 14.3 %copy-start.5 = (f32[16,256,128]{2,1,0:T(8,128)}, f32[16,256,128]{2,1,0:T(8,128)S(1)}, u32[]{:S(2)}) copy-start(f32[16,256,128]{2,1,0:T(8,128)S(1)} %get-tuple-element.36) | copy-start | bytes 6291460
  18.5 1.3 copy-start.3
  19.8 18.1 %collective-permute-start.2 = (f32[2,256,128]{2,1,0:T(8,128)S(1)}, f32[2,256,128]{2,1,0:T(8,128)S(1)}, u32[]{:S(2)}, u32[]{:S(2)}) collective-permute-start(f32[2,256,128]{2,1,0:T(8,128)S(1)} %slice.105), channel_id=1, source_target_pairs={{1,0},{2,1},{3,2},{4,3},{5,4},{6,5},{7,6},{9,8},{10,9},{11,10},{12... | collective-permute-start | bytes 786440 | tf_op jit(solution)/shard_map/ppermute | solution.py:12
  33.6 2.6 %copy-start.12 = (f32[3,16]{1,0:T(4,128)S(1)}, f32[3,16]{1,0:T(4,128)}, u32[]{:S(2)}) copy-start(f32[3,16]{1,0:T(4,128)} %param.13) | copy-start | bytes 580
  34.8 8.5 %collective-permute-start = (f32[2,256,128]{2,1,0:T(8,128)}, f32[2,256,128]{2,1,0:T(8,128)S(1)}, u32[]{:S(2)}, u32[]{:S(2)}) collective-permute-start(f32[2,256,128]{2,1,0:T(8,128)} %slice.74), channel_id=1, source_target_pairs={{1,0},{2,1},{3,2},{4,3},{5,4},{6,5},{7,6},{9,8},{10,9},{11,10},{12... | collective-permute-start | bytes 786440 | tf_op jit(solution)/shard_map/ppermute | solution.py:12
  41.7 2.5 %copy-start.6 = (f32[16,256,128]{2,1,0:T(8,128)S(1)}, f32[16,256,128]{2,1,0:T(8,128)}, u32[]{:S(2)}) copy-start(f32[16,256,128]{2,1,0:T(8,128)} %copy-done.5) | copy-start | bytes 6291460
  44.4 2.2 %copy-start.2 = (f32[18,256,128]{2,1,0:T(8,128)}, f32[18,256,128]{2,1,0:T(8,128)S(1)}, u32[]{:S(2)}) copy-start(f32[18,256,128]{2,1,0:T(8,128)S(1)} %pad_maximum_fusion) | copy-start | bytes 7077892
  50.9 11.4 %collective-permute-start.3 = (f32[18,258,1]{1,2,0:T(1,128)S(1)}, f32[18,258,1]{1,2,0:T(1,128)S(1)}, u32[]{:S(2)}, u32[]{:S(2)}) collective-permute-start(f32[18,258,1]{1,2,0:T(1,128)S(1)} %copy.33), channel_id=1, source_target_pairs={{8,0},{16,8},{24,16},{9,1},{17,9},{25,17},{10,2},{18,10},{26,18},{... | collective-permute-start | bytes 55736 | tf_op jit(solution)/shard_map/ppermute | solution.py:12
  54.9 5.3 %copy-start.7 = (f32[16,256,128]{2,1,0:T(8,128)S(1)}, f32[16,256,128]{2,1,0:T(8,128)}, u32[]{:S(2)}) copy-start(f32[16,256,128]{2,1,0:T(8,128)} %copy-done.5) | copy-start | bytes 6291460
  54.9 11.8 %collective-permute-start.1 = (f32[18,258,1]{1,2,0:T(1,128)S(1)}, f32[18,258,1]{1,2,0:T(1,128)S(1)}, u32[]{:S(2)}, u32[]{:S(2)}) collective-permute-start(f32[18,258,1]{1,2,0:T(1,128)S(1)} %copy.30), channel_id=1, source_target_pairs={{8,0},{16,8},{24,16},{9,1},{17,9},{25,17},{10,2},{18,10},{26,18},{... | collective-permute-start | bytes 55736 | tf_op jit(solution)/shard_map/ppermute | solution.py:12
  66.8 4.3 %copy-start.10 = (f32[1,256,128]{2,0,1:T(1,128)S(1)}, f32[1,256,128]{2,0,1:T(1,128)}, u32[]{:S(2)}) copy-start(f32[1,256,128]{2,0,1:T(1,128)} %get-tuple-element.40) | copy-start | bytes 393220
  66.8 4.3 %copy-start.11 = (f32[1,256,128]{2,0,1:T(1,128)S(1)}, f32[1,256,128]{2,0,1:T(1,128)}, u32[]{:S(2)}) copy-start(f32[1,256,128]{2,0,1:T(1,128)} %get-tuple-element.41) | copy-start | bytes 393220
  83.2 9.0 %copy-start.4 = (f32[16,256,128]{2,1,0:T(8,128)S(1)}, f32[16,256,128]{2,1,0:T(8,128)}, u32[]{:S(2)}) copy-start(f32[16,256,128]{2,1,0:T(8,128)} %copy-done.3) | copy-start | bytes 6291460
  85.5 13.4 %all-to-all-start = ((f32[1,256,128]{2,0,1:T(1,128)}), f32[1,256,128]{2,0,1:T(1,128)S(1)}, u32[]{:S(2)}, u32[]{:S(2)}) async-start(f32[1,256,128]{2,0,1:T(1,128)} %bitcast.7), calls=%async_computation | async-start | bytes 262144 | tf_op jit(solution)/shard_map/all_to_all | solution.py:103
  94.7 9.5 %copy-start.8 = (f32[16,256,128]{2,1,0:T(8,128)S(1)}, f32[16,256,128]{2,1,0:T(8,128)}, u32[]{:S(2)}) copy-start(f32[16,256,128]{2,1,0:T(8,128)} %get-tuple-element.38) | copy-start | bytes 6291460
  98.9 53.4 %all-to-all-start.2 = ((f32[16,256,128]{2,0,1:T(8,128)}), f32[16,256,128]{2,0,1:T(8,128)}, u32[]{:S(2)}, u32[]{:S(2)}) async-start(f32[16,256,128]{2,0,1:T(8,128)} %copy.36), calls=%async_computation.2 | async-start | bytes 4194304 | tf_op jit(solution)/shard_map/all_to_all | solution.py:121
  106.7 1.7 copy-start.9
  152.3 10.1 %all-to-all-start.1 = ((f32[1,256,128]{2,0,1:T(1,128)}), f32[1,256,128]{2,0,1:T(1,128)S(1)}, u32[]{:S(2)}, u32[]{:S(2)}) async-start(f32[1,256,128]{2,0,1:T(1,128)} %bitcast.14), calls=%async_computation.1 | async-start | bytes 262144 | tf_op jit(solution)/shard_map/all_to_all | solution.py:102
  162.4 31.5 %all-to-all-start.3 = ((f32[128,32,128]{2,1,0:T(8,128)}), f32[128,32,128]{2,1,0:T(8,128)S(1)}, u32[]{:S(2)}, u32[]{:S(2)}) async-start(f32[128,32,128]{2,1,0:T(8,128)} %bitcast.19), calls=%async_computation.3 | async-start | bytes 4194304 | tf_op jit(solution)/shard_map/all_to_all | solution.py:122
  169.4 26.2 %copy-start.1 = (s32[256,512]{1,0:T(8,128)S(1)}, s32[256,512]{1,0:T(8,128)}, u32[]{:S(2)}) copy-start(s32[256,512]{1,0:T(8,128)} %param.12) | copy-start | bytes 1572868
where the time goes:
time: 197 us; the launch traced here: 196 us
  waiting for transfers between devices  73.3 us (37%)
  local copies, waits for them, and re-layouts  47.3 us (24%)
  other arithmetic  30.4 us (15%)
  starting transfers between devices  26.8 us (14%)
  blocking collectives  9.72 us (5%)
  matrix products  7 us (4%)
    all_to_all x1, waiting for transfers between devices, local(): lax.all_to_all(lit, 'screen', split_axis=1, concat_axis=0, tiled=True)  42.7 us
    all_to_all x1, waiting for transfers between devices, local(): lax.all_to_all(lit_cam, 'light', split_axis=0, concat_axis=2, tiled=True)  23.3 us
    add x1, other arithmetic, resample(): mixed = near + light_w * (further - near)  12 us
    reshape x1, local copies, waits for them, and re-layouts, local(): density.reshape(bricks_b, BRICK, bricks_a, BRICK, bricks_l, BRICK)  10.6 us
    all_gather x1, blocking collectives, carried_in(): gathered = lax.all_gather(part, axis)  9.72 us
    slice x4, local copies, waits for them, and re-layouts, march_slabs(): tails = passed_along((dens_ext[:, :, :1], lit_ext[:, :, :1]), 'light', -1)  8.64 us
    all_to_all x1, starting transfers between devices, local(): lax.all_to_all(lit_cam, 'light', split_axis=0, concat_axis=2, tiled=True)  6.94 us
    all_to_all x1, starting transfers between devices, march_slabs(): lax.all_to_all(total[None], 'screen', split_axis=1, concat_axis=0, tiled=...  6.67 us
  transfers between devices with their start and end apart: 8, of which 4 were waited for; matrix products, arithmetic and copies ran while one was open for 24% of the time, Pallas kernels for 0%

commit v1 on v0

--- a/solution.py
+++ b/solution.py
@@ -4,6 +4,18 @@
 from jax.sharding import PartitionSpec as P
 
 BRICK = 16
+
+
+def measure_sites(shard_in, at_axis, own_rows):
+    z2, s_next = (shard_in.shape[:at_axis], shard_in.shape[at_axis + 1 :])
+    g_now = shard_in.reshape(*z2, own_rows, -1, *s_next)
+    return jnp.moveaxis(g_now, at_axis, 0)
+
+
+def review_the_state(view, which_dim):
+    t1 = list(view.shape[1:])
+    t1[which_dim] *= view.shape[0]
+    return jnp.moveaxis(view, 0, which_dim).reshape(t1)
 
 
 def passed_along(value, axis, by):
@@ -118,7 +130,20 @@
     before = carried_in(totals, "light", jnp.add, jnp.zeros_like(totals))
     incoming = lax.dynamic_slice_in_dim(light_in, screen_idx * slab_b, slab_b, 0)
     lit = albedo * incoming[:, :, None] * jnp.exp(-(local_depth + before[:, :, None]))
-    lit_cam = lax.all_to_all(lit, "screen", split_axis=1, concat_axis=0, tiled=True)
+    part_now = lax.axis_size("screen")
+    view_out = lax.axis_index("screen")
+    clean, local_part = (part_now, view_out)
+    a_next = measure_sites(lit, 1, clean)
+    chunks = [a_next[local_part]]
+    for d in range(1, clean):
+        tall = a_next[(local_part + d) % clean]
+        moved = lax.ppermute(
+            tall, "screen", perm=[(dev_i, (dev_i + d) % clean) for dev_i in range(clean)]
+        )
+        chunks.append(moved)
+    v_now = jnp.stack(chunks, 0)
+    a_next = v_now[(local_part - jnp.arange(clean)) % clean]
+    lit_cam = review_the_state(a_next, 0)
     lit_cam = lax.all_to_all(lit_cam, "light", split_axis=0, concat_axis=2, tiled=True)
     picture, passing = march_slabs(masked, lit, phase, fractions)
     return (picture, passing, lit_cam)

time: 197 us -> 177 us (0.90)
  waiting for transfers between devices: 73.3 us -> 36.3 us
  local copies, waits for them, and re-layouts: 47.3 us -> 60.7 us
  starting transfers between devices: 26.8 us -> 34.4 us
  other arithmetic: 30.4 us -> 27.2 us
    all_to_all x1 -> x0, waiting for transfers between devices: 42.7 us -> none  [local(): lax.all_to_all(lit, 'screen', split_axis=1, concat_axis=0, tiled=True)]
    ppermute x0 -> x7, starting transfers between devices: none -> 14 us  [local(): lax.ppermute(tall, 'screen', perm=[(dev_i, (dev_i + d) % clean) for dev_i...]
    ppermute x0 -> x7, waiting for transfers between devices: none -> 10.3 us  [local(): lax.ppermute(tall, 'screen', perm=[(dev_i, (dev_i + d) % clean) for dev_i...]
    unnamed x27 -> x30, local copies, waits for them, and re-layouts: 3.87 us -> 10.7 us
    all_to_all x1 -> x0, starting transfers between devices: 4.36 us -> none  [local(): lax.all_to_all(lit, 'screen', split_axis=1, concat_axis=0, tiled=True)]
    gather x0 -> x1, local copies, waits for them, and re-layouts: none -> 3.59 us  [local(): a_next = v_now[(local_part - jnp.arange(clean)) % clean]]
    all_to_all x1 -> x0, local copies, waits for them, and re-layouts: 3.54 us -> none  [local(): lax.all_to_all(lit, 'screen', split_axis=1, concat_axis=0, tiled=True)]
    all_to_all x1, waiting for transfers between devices: 4.2 us -> 1.28 us  [march_slabs(): lax.all_to_all(total[None], 'screen', split_axis=1, concat_axis=0, tiled=...]
  transfers between devices with their start and end apart: 8 -> 14, of which waited for: 4 -> 5; matrix products, arithmetic and copies ran while one was open for 24% -> 46% of each run, Pallas kernels for 0% -> 0%
where the time goes in v1:
time: 177 us; the launch traced here: 176 us
  local copies, waits for them, and re-layouts  60.7 us (34%)
  waiting for transfers between devices  36.3 us (21%)
  starting transfers between devices  34.4 us (19%)
  other arithmetic  27.2 us (15%)
  blocking collectives  9.71 us (5%)
  matrix products  6.73 us (4%)
    all_to_all x1, waiting for transfers between devices, local(): lax.all_to_all(lit_cam, 'light', split_axis=0, concat_axis=2, tiled=True)  23.3 us
    ppermute x7, starting transfers between devices, local(): lax.ppermute(tall, 'screen', perm=[(dev_i, (dev_i + d) % clean) for dev_i...  14 us
    add x1, other arithmetic, resample(): mixed = near + light_w * (further - near)  12 us
    unnamed x30, local copies, waits for them, and re-layouts  10.7 us
    reshape x1, local copies, waits for them, and re-layouts, local(): density.reshape(bricks_b, BRICK, bricks_a, BRICK, bricks_l, BRICK)  10.5 us
    ppermute x7, waiting for transfers between devices, local(): lax.ppermute(tall, 'screen', perm=[(dev_i, (dev_i + d) % clean) for dev_i...  10.3 us
    slice x4, local copies, waits for them, and re-layouts, march_slabs(): tails = passed_along((dens_ext[:, :, :1], lit_ext[:, :, :1]), 'light', -1)  9.92 us
    all_gather x1, blocking collectives, carried_in(): gathered = lax.all_gather(part, axis)  9.71 us
  transfers between devices with their start and end apart: 14, of which 5 were waited for; matrix products, arithmetic and copies ran while one was open for 46% of the time, Pallas kernels for 0%

profile of v1, /device:TPU:0, one launch (start us, length us, event | category | flops | bytes accessed | tf_op | source)
XLA Modules:
  0.0 176.1 jit_solution(16131449961681536945)
XLA Ops:
  2.7 1.5 mul.121
  4.2 1.8 %fusion.37 = (f32[16,256]{1,0:T(8,128)S(1)}, f32[16,256,128]{2,1,0:T(8,128)}) fusion(f32[16,256,128]{2,1,0:T(8,128)S(1)} %copy-done.8, f32[256,128]{1,0:T(8,128)S(1)} %mul.121), kind=kLoop, calls=%fused_computation.85 | loop fusion | flops 1044480 | bytes 4341760 | tf_op jit(solution)/shard_map/reduce_sum | solution.py:47
  6.0 9.7 %all-gather = f32[64,256]{1,0:T(8,128)S(1)} all-gather(f32[16,256]{1,0:T(8,128)S(1)} %get-tuple-element.35), channel_id=2, replica_groups=mesh['light'=4,'screen'=8] {'light'}, dimensions={0}, use_global_device_ids=true | all-gather | bytes 81920 | tf_op jit(solution)/shard_map/all_gather | solution.py:29
  16.5 3.6 %exponential_multiply_fusion = f32[16,256,128]{2,1,0:T(8,128)S(1)} fusion(f32[16,256,128]{2,1,0:T(8,128)} %param.9, f32[16,256,128]{2,1,0:T(8,128)} %get-tuple-element.36, f32[16,256]{1,0:T(8,128)S(1)} %get-tuple-element.26, f32[16,256]{1,0:T(8,128)S(1)} %sub.79, f32[16,256]{1,0:T(8,128)S(1)} %constant_dynamic-slice_fusion), kind=kOutput, calls=%fused_computation.43 | convolution fusion | flops 807944192 | bytes 6340608 | tf_op jit(solution)/shard_map/dot_general | solution.py:46
  20.8 1.3 collective-permute-start.2
  22.2 1.3 dynamic-slice_bitcast_fusion
  23.5 4.3 %collective-permute-start.10 = (f32[16,32,128]{2,1,0:T(8,128)}, f32[16,32,128]{2,1,0:T(8,128)}, u32[]{:S(2)}, u32[]{:S(2)}) collective-permute-start(f32[16,32,128]{2,1,0:T(8,128)} %get-tuple-element.39), channel_id=1, source_target_pairs={{0,7},{1,0},{2,1},{3,2},{4,3},{5,4},{6,5},{7,6},{8,15},{9,8},{10,9... | collective-permute-start | bytes 786440 | tf_op jit(solution)/shard_map/ppermute | solution.py:140
  28.9 10.5 %reshape.152 = f32[1,16,16,16,8,16]{5,4,3,2,1,0:T(8,128)} reshape(f32[16,256,128]{2,1,0:T(8,128)} %param.8) | data formatting | bytes 4194304 | tf_op jit(solution)/shard_map/reshape | solution.py:124
  40.2 1.9 %slice_multiply_fusion = f32[1,2,16,16,8,16]{5,4,3,2,1,0:T(8,128)S(1)} fusion(f32[1,16,16,16,8,16]{5,4,3,2,1,0:T(8,128)} %reshape.152, f32[16,8]{1,0:T(8,128)S(1)} %copy.16), kind=kLoop, calls=%fused_computation.42 | loop fusion | flops 65536 | bytes 524800 | tf_op jit(solution)/shard_map/mul | solution.py:124
  42.8 1.3 slice.74
  44.4 1.3 collective-permute-start
  45.7 1.7 pad_maximum_fusion.1
  47.5 1.6 pad_slice_fusion.3
  49.1 4.2 %collective-permute-start.5 = (f32[16,32,128]{2,1,0:T(8,128)S(1)}, f32[16,32,128]{2,1,0:T(8,128)S(1)}, u32[]{:S(2)}, u32[]{:S(2)}) collective-permute-start(f32[16,32,128]{2,1,0:T(8,128)S(1)} %copy-done.9), channel_id=1, source_target_pairs={{0,2},{1,3},{2,4},{3,5},{4,6},{5,7},{6,0},{7,1},{8,10},{9,11},{10,... | collective-permute-start | bytes 786440 | tf_op jit(solution)/shard_map/ppermute | solution.py:140
  53.5 1.5 collective-permute-start.7
  55.0 1.7 bitcast_dynamic-update-slice_fusion.6
  56.7 2.9 %collective-permute-done.5 = f32[16,32,128]{2,1,0:T(8,128)S(1)} collective-permute-done((f32[16,32,128]{2,1,0:T(8,128)S(1)}, f32[16,32,128]{2,1,0:T(8,128)S(1)}, u32[]{:S(2)}, u32[]{:S(2)}) %collective-permute-start.5) | collective-permute-done | bytes 262176 | tf_op jit(solution)/shard_map/ppermute | solution.py:140
  59.6 3.0 %collective-permute-start.6 = (f32[16,32,128]{2,1,0:T(8,128)}, f32[16,32,128]{2,1,0:T(8,128)}, u32[]{:S(2)}, u32[]{:S(2)}) collective-permute-start(f32[16,32,128]{2,1,0:T(8,128)} %get-tuple-element.43), channel_id=1, source_target_pairs={{0,3},{1,4},{2,5},{3,6},{4,7},{5,0},{6,1},{7,2},{8,11},{9,12},{10,... | collective-permute-start | bytes 786440 | tf_op jit(solution)/shard_map/ppermute | solution.py:140
  63.3 1.6 pad_slice_fusion.5
  64.9 2.2 %pad_slice_fusion.2 = f32[18,256,127]{2,1,0:T(8,128)} fusion(f32[18,256,128]{2,1,0:T(8,128)S(1)} %pad_maximum_fusion.1), kind=kLoop, calls=%fused_computation.26 | loop fusion | bytes 4700160 | tf_op jit(solution)/shard_map/slice | solution.py:77
  67.1 3.3 %copy.21 = f32[18,258,1]{1,2,0:T(1,128)} copy(f32[18,258,1]{2,1,0:T(8,128)} %pad_slice_fusion.3) | data formatting | bytes 37152 | tf_op jit(solution)/shard_map/slice | solution.py:107
  70.4 3.3 %copy.18 = f32[18,258,1]{1,2,0:T(1,128)} copy(f32[18,258,1]{2,1,0:T(8,128)} %pad_slice_fusion.5) | data formatting | bytes 37152 | tf_op jit(solution)/shard_map/slice | solution.py:107
  73.7 7.4 %collective-permute-done.6 = f32[16,32,128]{2,1,0:T(8,128)} collective-permute-done((f32[16,32,128]{2,1,0:T(8,128)}, f32[16,32,128]{2,1,0:T(8,128)}, u32[]{:S(2)}, u32[]{:S(2)}) %collective-permute-start.6) | collective-permute-done | bytes 262176 | tf_op jit(solution)/shard_map/ppermute | solution.py:140
  81.1 1.3 collective-permute-start.3
  82.4 1.7 bitcast_dynamic-update-slice_fusion.4
  84.1 1.5 collective-permute-start.1
  86.3 3.9 %pad_slice_fusion.4 = f32[18,256,127]{2,1,0:T(8,128)} fusion(f32[18,256,128]{2,1,0:T(8,128)} %copy-done.2), kind=kLoop, calls=%fused_computation.28 | loop fusion | bytes 4700160 | tf_op jit(solution)/shard_map/slice | solution.py:77
  90.2 2.1 %fusion.3 = f32[18,256,127]{2,1,0:T(8,128)} fusion(f32[2,256,128]{2,1,0:T(8,128)S(1)} %collective-permute-done.2, f32[16,256,128]{2,1,0:T(8,128)S(1)} %copy-done.4), kind=kLoop, calls=%fused_computation.10 | loop fusion | flops 585216 | bytes 4700160 | tf_op jit(solution)/shard_map/concatenate | solution.py:106
  92.3 1.7 bitcast_dynamic-update-slice_fusion.2
  94.0 1.7 bitcast_dynamic-update-slice_fusion.1
  95.7 2.1 %fusion.4 = f32[18,256,127]{2,1,0:T(8,128)} fusion(f32[2,256,128]{2,1,0:T(8,128)S(1)} %collective-permute-done, f32[16,256,128]{2,1,0:T(8,128)S(1)} %copy-done.6), kind=kLoop, calls=%fused_computation.11 | loop fusion | flops 585216 | bytes 4700160 | tf_op jit(solution)/shard_map/concatenate | solution.py:105
  97.9 2.1 %copy.23 = f32[18,256,1]{2,1,0:T(8,128)} copy(f32[18,256,1]{1,2,0:T(1,128)S(1)} %get-tuple-element.51) | data formatting | bytes 36864 | tf_op jit(solution)/shard_map/slice | solution.py:75
  100.0 2.2 %copy.22 = f32[18,256,1]{2,1,0:T(8,128)} copy(f32[18,256,1]{1,2,0:T(1,128)S(1)} %get-tuple-element.52) | data formatting | bytes 36864 | tf_op jit(solution)/shard_map/slice | solution.py:74
  103.1 2.1 %copy.20 = f32[18,256,1]{2,1,0:T(8,128)} copy(f32[18,256,1]{1,2,0:T(1,128)S(1)} %get-tuple-element.53) | data formatting | bytes 36864 | tf_op jit(solution)/shard_map/slice | solution.py:75
  105.2 2.1 %copy.19 = f32[18,256,1]{2,1,0:T(8,128)} copy(f32[18,256,1]{1,2,0:T(1,128)S(1)} %get-tuple-element.54) | data formatting | bytes 36864 | tf_op jit(solution)/shard_map/slice | solution.py:74
  107.3 12.0 %fusion.14 = (f32[18,256,128]{2,1,0:T(8,128)}, f32[18,256,128]{2,1,0:T(8,128)S(1)}) fusion(f32[18,256,1]{2,1,0:T(8,128)} %copy.22, f32[18,256,127]{2,1,0:T(8,128)} %fusion.3, f32[18,256,1]{2,1,0:T(8,128)} %copy.23, f32[18,256,127]{2,1,0:T(8,128)} %pad_slice_fusion.2, f32[18,256,128]{2,1,0:T(8,128)S(1)} %pad_maximum_fusion.1, f32[256,128]{1,0:T(8,128)S(1)} %bitcast.106, ...), kind=kLoop, calls=%fused_computation.25 | loop fusion | flops 12976128 | bytes 19136512 | tf_op jit(solution)/shard_map/add | solution.py:83
  121.3 3.9 %all-to-all-start = ((f32[1,256,128]{2,0,1:T(1,128)}), f32[1,256,128]{2,0,1:T(1,128)S(1)}, u32[]{:S(2)}, u32[]{:S(2)}) async-start(f32[1,256,128]{2,0,1:T(1,128)} %bitcast.7), calls=%async_computation | async-start | bytes 262144 | tf_op jit(solution)/shard_map/all_to_all | solution.py:115
  125.3 2.5 %fusion.24 = f32[2,8,256,128]{3,1,2,0:T(8,128)S(1)} fusion(f32[2,8,256,128]{3,2,1,0:T(8,128)S(1)} %bitcast.99, f32[32768]{0:T(1024)S(1)} %subtract_bitcast_fusion), kind=kOutput, calls=%fused_computation.46 | convolution fusion | flops 101712128 | bytes 4325376 | tf_op jit(solution)/shard_map/ij,bjr->bir/dot_general | solution.py:59
  128.2 1.2 copy-done.7
  129.4 1.3 fusion.16
  130.7 1.3 all-to-all-done
  132.0 3.8 %all-to-all-start.1 = ((f32[1,256,128]{2,0,1:T(1,128)}), f32[1,256,128]{2,0,1:T(1,128)S(1)}, u32[]{:S(2)}, u32[]{:S(2)}) async-start(f32[1,256,128]{2,0,1:T(1,128)} %bitcast.14), calls=%async_computation.1 | async-start | bytes 262144 | tf_op jit(solution)/shard_map/all_to_all | solution.py:114
  135.8 1.7 bitcast_dynamic-update-slice_fusion
  137.5 3.6 %gather_fusion = f32[8,16,32,128]{3,2,1,0:T(8,128)} fusion(f32[8,16,32,128]{3,2,1,0:T(8,128)} %bitcast_dynamic-update-slice_fusion, s32[1024]{0:T(1024)S(1)} %pad_clamp_fusion), kind=kCustom, calls=%fused_computation | custom fusion | bytes 4194336 | tf_op jit(solution)/shard_map/gather | solution.py:145
  141.1 1.5 all-to-all-done.1
  142.6 7.4 %all-to-all-start.2 = ((f32[128,32,128]{2,1,0:T(8,128)}), f32[128,32,128]{2,1,0:T(8,128)S(1)}, u32[]{:S(2)}, u32[]{:S(2)}) async-start(f32[128,32,128]{2,1,0:T(8,128)} %bitcast.33), calls=%async_computation.2 | async-start | bytes 4194304 | tf_op jit(solution)/shard_map/all_to_all | solution.py:147
  151.2 23.3 %all-to-all-done.2 = f32[128,32,128]{2,1,0:T(8,128)S(1)} async-done(((f32[128,32,128]{2,1,0:T(8,128)}), f32[128,32,128]{2,1,0:T(8,128)S(1)}, u32[]{:S(2)}, u32[]{:S(2)}) %all-to-all-start.2) | async-done | bytes 2097184 | tf_op jit(solution)/shard_map/all_to_all | solution.py:147
  174.5 1.6 copy.35
  (58 shorter events, 12.7 us)
Async XLA Ops:
  0.6 41.4 %copy-start = (s32[256,512]{1,0:T(8,128)S(1)}, s32[256,512]{1,0:T(8,128)}, u32[]{:S(2)}) copy-start(s32[256,512]{1,0:T(8,128)} %param.12) | copy-start | bytes 1572868
  0.6 3.6 %copy-start.8 = (f32[16,256,128]{2,1,0:T(8,128)S(1)}, f32[16,256,128]{2,1,0:T(8,128)}, u32[]{:S(2)}) copy-start(f32[16,256,128]{2,1,0:T(8,128)} %param.8) | copy-start | bytes 6291460
  20.1 19.4 %copy-start.3 = (f32[16,256,128]{2,1,0:T(8,128)}, f32[16,256,128]{2,1,0:T(8,128)S(1)}, u32[]{:S(2)}) copy-start(f32[16,256,128]{2,1,0:T(8,128)S(1)} %exponential_multiply_fusion) | copy-start | bytes 6291460
  20.8 23.6 %collective-permute-start.2 = (f32[2,256,128]{2,1,0:T(8,128)}, f32[2,256,128]{2,1,0:T(8,128)S(1)}, u32[]{:S(2)}, u32[]{:S(2)}) collective-permute-start(f32[2,256,128]{2,1,0:T(8,128)} %slice.107), channel_id=1, source_target_pairs={{1,0},{2,1},{3,2},{4,3},{5,4},{6,5},{7,6},{9,8},{10,9},{11,10},{12... | collective-permute-start | bytes 786440 | tf_op jit(solution)/shard_map/ppermute | solution.py:24
  23.5 112.3 %collective-permute-start.10 = (f32[16,32,128]{2,1,0:T(8,128)}, f32[16,32,128]{2,1,0:T(8,128)}, u32[]{:S(2)}, u32[]{:S(2)}) collective-permute-start(f32[16,32,128]{2,1,0:T(8,128)} %get-tuple-element.39), channel_id=1, source_target_pairs={{0,7},{1,0},{2,1},{3,2},{4,3},{5,4},{6,5},{7,6},{8,15},{9,8},{10,9... | collective-permute-start | bytes 786440 | tf_op jit(solution)/shard_map/ppermute | solution.py:140
  27.9 66.1 %collective-permute-start.9 = (f32[16,32,128]{2,1,0:T(8,128)}, f32[16,32,128]{2,1,0:T(8,128)}, u32[]{:S(2)}, u32[]{:S(2)}) collective-permute-start(f32[16,32,128]{2,1,0:T(8,128)} %get-tuple-element.40), channel_id=1, source_target_pairs={{0,6},{1,7},{2,0},{3,1},{4,2},{5,3},{6,4},{7,5},{8,14},{9,15},{10,... | collective-permute-start | bytes 786440 | tf_op jit(solution)/shard_map/ppermute | solution.py:140
  28.3 64.0 %collective-permute-start.8 = (f32[16,32,128]{2,1,0:T(8,128)}, f32[16,32,128]{2,1,0:T(8,128)}, u32[]{:S(2)}, u32[]{:S(2)}) collective-permute-start(f32[16,32,128]{2,1,0:T(8,128)} %get-tuple-element.41), channel_id=1, source_target_pairs={{0,5},{1,6},{2,7},{3,0},{4,1},{5,2},{6,3},{7,4},{8,13},{9,14},{10,... | collective-permute-start | bytes 786440 | tf_op jit(solution)/shard_map/ppermute | solution.py:140
  28.3 25.2 %collective-permute-start.4 = (f32[16,32,128]{2,1,0:T(8,128)}, f32[16,32,128]{2,1,0:T(8,128)}, u32[]{:S(2)}, u32[]{:S(2)}) collective-permute-start(f32[16,32,128]{2,1,0:T(8,128)} %get-tuple-element.45), channel_id=1, source_target_pairs={{0,1},{1,2},{2,3},{3,4},{4,5},{5,6},{6,7},{7,0},{8,9},{9,10},{10,1... | collective-permute-start | bytes 786440 | tf_op jit(solution)/shard_map/ppermute | solution.py:140
  40.2 1.9 %copy-start.10 = (f32[3,16]{1,0:T(4,128)S(1)}, f32[3,16]{1,0:T(4,128)}, u32[]{:S(2)}) copy-start(f32[3,16]{1,0:T(4,128)} %param.13) | copy-start | bytes 580
  44.4 4.7 %collective-permute-start = (f32[2,256,128]{2,1,0:T(8,128)}, f32[2,256,128]{2,1,0:T(8,128)S(1)}, u32[]{:S(2)}, u32[]{:S(2)}) collective-permute-start(f32[2,256,128]{2,1,0:T(8,128)} %slice.74), channel_id=1, source_target_pairs={{1,0},{2,1},{3,2},{4,3},{5,4},{6,5},{7,6},{9,8},{10,9},{11,10},{12... | collective-permute-start | bytes 786440 | tf_op jit(solution)/shard_map/ppermute | solution.py:24
  47.4 1.7 copy-start.9
  47.4 5.8 %copy-start.5 = (f32[16,256,128]{2,1,0:T(8,128)S(1)}, f32[16,256,128]{2,1,0:T(8,128)}, u32[]{:S(2)}) copy-start(f32[16,256,128]{2,1,0:T(8,128)} %get-tuple-element.36) | copy-start | bytes 6291460
  49.1 10.5 %collective-permute-start.5 = (f32[16,32,128]{2,1,0:T(8,128)S(1)}, f32[16,32,128]{2,1,0:T(8,128)S(1)}, u32[]{:S(2)}, u32[]{:S(2)}) collective-permute-start(f32[16,32,128]{2,1,0:T(8,128)S(1)} %copy-done.9), channel_id=1, source_target_pairs={{0,2},{1,3},{2,4},{3,5},{4,6},{5,7},{6,0},{7,1},{8,10},{9,11},{10,... | collective-permute-start | bytes 786440 | tf_op jit(solution)/shard_map/ppermute | solution.py:140
  53.5 11.4 %copy-start.2 = (f32[18,256,128]{2,1,0:T(8,128)}, f32[18,256,128]{2,1,0:T(8,128)S(1)}, u32[]{:S(2)}) copy-start(f32[18,256,128]{2,1,0:T(8,128)S(1)} %pad_maximum_fusion) | copy-start | bytes 7077892
  53.5 30.6 %collective-permute-start.7 = (f32[16,32,128]{2,1,0:T(8,128)}, f32[16,32,128]{2,1,0:T(8,128)S(1)}, u32[]{:S(2)}, u32[]{:S(2)}) collective-permute-start(f32[16,32,128]{2,1,0:T(8,128)} %get-tuple-element.42), channel_id=1, source_target_pairs={{0,4},{1,5},{2,6},{3,7},{4,0},{5,1},{6,2},{7,3},{8,12},{9,13},{10,... | collective-permute-start | bytes 786440 | tf_op jit(solution)/shard_map/ppermute | solution.py:140
  59.6 21.5 %collective-permute-start.6 = (f32[16,32,128]{2,1,0:T(8,128)}, f32[16,32,128]{2,1,0:T(8,128)}, u32[]{:S(2)}, u32[]{:S(2)}) collective-permute-start(f32[16,32,128]{2,1,0:T(8,128)} %get-tuple-element.43), channel_id=1, source_target_pairs={{0,3},{1,4},{2,5},{3,6},{4,7},{5,0},{6,1},{7,2},{8,11},{9,12},{10,... | collective-permute-start | bytes 786440 | tf_op jit(solution)/shard_map/ppermute | solution.py:140
  81.1 16.7 %collective-permute-start.3 = (f32[18,258,1]{1,2,0:T(1,128)}, f32[18,258,1]{1,2,0:T(1,128)S(1)}, u32[]{:S(2)}, u32[]{:S(2)}) collective-permute-start(f32[18,258,1]{1,2,0:T(1,128)} %copy.21), channel_id=1, source_target_pairs={{8,0},{16,8},{24,16},{9,1},{17,9},{25,17},{10,2},{18,10},{26,18},{... | collective-permute-start | bytes 55736 | tf_op jit(solution)/shard_map/ppermute | solution.py:24
  84.1 18.1 %collective-permute-start.1 = (f32[18,258,1]{1,2,0:T(1,128)}, f32[18,258,1]{1,2,0:T(1,128)}, u32[]{:S(2)}, u32[]{:S(2)}) collective-permute-start(f32[18,258,1]{1,2,0:T(1,128)} %copy.18), channel_id=1, source_target_pairs={{8,0},{16,8},{24,16},{9,1},{17,9},{25,17},{10,2},{18,10},{26,18},{... | collective-permute-start | bytes 55736 | tf_op jit(solution)/shard_map/ppermute | solution.py:24
  86.3 3.9 %copy-start.4 = (f32[16,256,128]{2,1,0:T(8,128)S(1)}, f32[16,256,128]{2,1,0:T(8,128)}, u32[]{:S(2)}) copy-start(f32[16,256,128]{2,1,0:T(8,128)} %copy-done.3) | copy-start | bytes 6291460
  90.2 5.5 %copy-start.6 = (f32[16,256,128]{2,1,0:T(8,128)S(1)}, f32[16,256,128]{2,1,0:T(8,128)}, u32[]{:S(2)}) copy-start(f32[16,256,128]{2,1,0:T(8,128)} %get-tuple-element.36) | copy-start | bytes 6291460
  121.3 10.7 %all-to-all-start = ((f32[1,256,128]{2,0,1:T(1,128)}), f32[1,256,128]{2,0,1:T(1,128)S(1)}, u32[]{:S(2)}, u32[]{:S(2)}) async-start(f32[1,256,128]{2,0,1:T(1,128)} %bitcast.7), calls=%async_computation | async-start | bytes 262144 | tf_op jit(solution)/shard_map/all_to_all | solution.py:115
  127.7 1.7 copy-start.7
  132.0 10.6 %all-to-all-start.1 = ((f32[1,256,128]{2,0,1:T(1,128)}), f32[1,256,128]{2,0,1:T(1,128)S(1)}, u32[]{:S(2)}, u32[]{:S(2)}) async-start(f32[1,256,128]{2,0,1:T(1,128)} %bitcast.14), calls=%async_computation.1 | async-start | bytes 262144 | tf_op jit(solution)/shard_map/all_to_all | solution.py:114
  142.6 31.9 %all-to-all-start.2 = ((f32[128,32,128]{2,1,0:T(8,128)}), f32[128,32,128]{2,1,0:T(8,128)S(1)}, u32[]{:S(2)}, u32[]{:S(2)}) async-start(f32[128,32,128]{2,1,0:T(8,128)} %bitcast.33), calls=%async_computation.2 | async-start | bytes 4194304 | tf_op jit(solution)/shard_map/all_to_all | solution.py:147
  174.5 1.6 copy-start.1
